TPU v7x, 256 devices: a 8x8x2 block of a 8x8x16 slice. The times are simulated.
256 devices in a mesh: parts: 2 (over z), node: 8 (over x), local: 16 (over y, core).
Axes of the slice: x: 8, y: 8, z: 2, core: 2. Of those that a mesh axis runs over, the one named last changes fastest.
The devices are a block of a 8x8x16 slice.
Arguments:
- tokens: bfloat16 [2048, 7168], P(('parts', 'node', 'local')), parts along dimension 0, may hold values from -6 to 6
- expert_ids: int32 [2048, 8], P(('parts', 'node', 'local')), parts along dimension 0, may hold values from 0 to 15, as said below
- gate_weights: bfloat16 [2048, 8], P(('parts', 'node', 'local')), parts along dimension 0, may hold values from 0.099609375 to 1
- slots: int32 [2048, 8], P(('parts', 'node', 'local')), parts along dimension 0, may hold values from 0 to 8, as said below
- w_gate: bfloat16 [32, 7168, 2048], P(('parts', 'node'), None, 'local'), parts along dimension 0, may hold values from -0.0625 to 0.0625
- w_up: bfloat16 [32, 7168, 2048], P(('parts', 'node'), None, 'local'), parts along dimension 0, may hold values from -0.0625 to 0.0625
- w_down: bfloat16 [32, 2048, 7168], P(('parts', 'node'), 'local'), parts along dimension 0, may hold values from -0.125 to 0.125
Outputs:
- combined: bfloat16 [2048, 7168], P(('parts', 'node', 'local')), parts along dimension 0
There are 2 independent parts, one for each index of `parts`. A program takes and returns all parts, laid end to end along the dimension named above; each array names one. Nothing has to cross between parts.
Inputs may be any that keep to these rules, and one draw needn't show every extreme that they name: `expert_ids`: each row names 8 different experts, all within at most 4 node groups; expert e belongs to node group e // 2. slots[t, n] is below 8 exactly where some expert of token t belongs to node group n, and equals 8 elsewhere; within each aligned block of 8 rows (the rows of one device) the values below 8 in one column are distinct.
All inputs are finite; a program needn't handle non-finite values.
Results may differ from a plain program's by a relative error of at most 0.019.
Values may be sent and summed in bfloat16 or wider, within the bound.
No kernel may reach another device: no remote copies, remote signals or barrier semaphores. Data moves between devices by JAX's collectives and lax.ppermute only.
A program may use at most 192 MiB of HBM per device.

v0:
```python
import functools

import jax
import jax.numpy as jnp
from jax import lax
from jax.experimental import pallas as pl
from jax.experimental.pallas import tpu as pltpu
from jax.sharding import Mesh, PartitionSpec as P


PLANE = ("node", "chip", "core")
LANES = 128
VMEM_LIMIT = 20 * 2**20


def place(chips, cores, x, y, c):
    return (x * chips + y) * cores + c


def shift_pairs(nodes, chips, cores, ring, step):
    pairs = []
    for x in range(nodes):
        for y in range(chips):
            for c in range(cores):
                along_x = (c == 0) != ring
                tx, ty = ((x + step) % nodes, y) if along_x else (x, (y + step) % chips)
                pairs.append((place(chips, cores, x, y, c), place(chips, cores, tx, ty, c)))
    return pairs


def expert_kernel(pieces, width, top, count, steps, steps_out, node_ref, *refs):
    x_refs, refs = refs[:pieces], refs[pieces:]
    w_gate, w_up, p_gate, p_up, w_down, p_down = refs[:6]
    out_refs, (acc, hid, *held, sems) = refs[6 : 6 + pieces], refs[6 + pieces :]
    per_node, _, units = w_gate.shape
    lanes = per_node * units
    block = width // steps
    copies = [
        pltpu.make_async_copy(source, buf, sems.at[i])
        for i, (source, buf) in enumerate(zip((p_gate, p_up, w_down, p_down), held))
    ]
    for copy in copies:
        copy.start()
    acc[...] = jnp.zeros_like(acc)

    def multiply_in(side, sources):
        @pl.loop(0, steps)
        def _(k):
            at = pl.ds(pl.multiple_of(k * block, block), block)
            x = jnp.concatenate([r[:, at] for r in x_refs], axis=0)
            for i, source in enumerate(sources):
                to = (2 * i + side) * lanes
                w = jnp.concatenate([source[m, at] for m in range(per_node)], axis=1)
                acc[:, to : to + lanes] += jnp.dot(x, w, preferred_element_type=jnp.float32)

    multiply_in(0, (w_gate, w_up))
    copies[0].wait()
    copies[1].wait()
    multiply_in(1, held[:2])

    meta = jnp.concatenate([r[:, width : width + LANES] for r in x_refs], axis=0)
    meta = meta.astype(jnp.float32)
    lane = lax.broadcasted_iota(jnp.int32, meta.shape, 1)
    weights = pltpu.roll(meta, LANES - top, 1)
    node = node_ref[0]
    slot = jnp.sum(jnp.where(lane == 2 * top + node, meta, 0.0), axis=1, keepdims=True)
    reached = jnp.where(slot < count, 1.0, 0.0)
    gates = []
    for m in range(per_node):
        expert = (node * per_node + m).astype(jnp.float32)
        hit = jnp.logical_and(lane < top, meta == expert)
        gates.append(jnp.sum(jnp.where(hit, weights, 0.0), axis=1, keepdims=True) * reached)
    for i in range(2):
        for m in range(per_node):
            at = i * lanes + m * units
            g = acc[:, at : at + units]
            u = acc[:, 2 * lanes + at : 2 * lanes + at + units]
            hid[:, at : at + units] = (gates[m] * (g / (1.0 + jnp.exp(-g)) * u)).astype(hid.dtype)

    copies[2].wait()
    copies[3].wait()
    ends = [0]
    for o in out_refs:
        ends.append(ends[-1] + o.shape[0])

    block = width // steps_out

    @pl.loop(0, steps_out)
    def _(k):
        at = pl.ds(pl.multiple_of(k * block, block), block)
        y = jnp.dot(
            hid[:, :lanes],
            held[2][:, :, at].reshape(lanes, block),
            preferred_element_type=jnp.float32,
        )
        y += jnp.dot(
            hid[:, lanes:],
            held[3][:, :, at].reshape(lanes, block),
            preferred_element_type=jnp.float32,
        )
        for j, o in enumerate(out_refs):
            o[:, at] = y[ends[j] : ends[j + 1]].astype(o.dtype)


def experts(node, pieces, weights, top, count):
    per_node, width, units = weights[0].shape
    lanes = per_node * units
    steps = next(n for n in (4, 7, 1) if width % (n * LANES) == 0)
    steps_out = next(n for n in (7, 4, 1) if width % (n * LANES) == 0)
    total = sum(p.shape[0] for p in pieces)
    vmem = pl.BlockSpec(memory_space=pltpu.VMEM)
    hbm = pl.BlockSpec(memory_space=pltpu.HBM)
    return pl.pallas_call(
        functools.partial(expert_kernel, len(pieces), width, top, count, steps, steps_out),
        out_shape=[jax.ShapeDtypeStruct((p.shape[0], width), p.dtype) for p in pieces],
        in_specs=[pl.BlockSpec(memory_space=pltpu.SMEM)] + [vmem] * (len(pieces) + 2) + [hbm] * 4,
        out_specs=[vmem] * len(pieces),
        scratch_shapes=[
            pltpu.VMEM((total, 4 * lanes), jnp.float32),
            pltpu.VMEM((total, 2 * lanes), weights[0].dtype),
            *[pltpu.VMEM(w.shape, w.dtype) for w in weights[2:]],
            pltpu.SemaphoreType.DMA((4,)),
        ],
        compiler_params=pltpu.CompilerParams(vmem_limit_bytes=VMEM_LIMIT),
        cost_estimate=pl.CostEstimate(
            flops=2 * total * width * 6 * lanes,
            bytes_accessed=4 * total * width,
            transcendentals=total * 2 * lanes,
        ),
        name="experts",
    )(node, *pieces, *weights)


def build(nodes, chips, cores):
    reach = nodes // 2

    def ring_move(x, step):
        return lax.ppermute(x, PLANE, shift_pairs(nodes, chips, cores, True, step))

    def line_move(x, step):
        return lax.ppermute(x, PLANE, shift_pairs(nodes, chips, cores, False, step))

    def add(a, b):
        return (a.astype(jnp.float32) + b.astype(jnp.float32)).astype(a.dtype)

    def local(tokens, expert_ids, gate_weights, slots, w_gate, w_up, w_down):
        count, _ = tokens.shape
        top = expert_ids.shape[1]
        node = lax.axis_index("node").astype(jnp.int32).reshape(1)

        meta = jnp.concatenate([a.astype(tokens.dtype) for a in (expert_ids, gate_weights, slots)], 1)
        meta = jnp.pad(meta, ((0, 0), (0, LANES - meta.shape[1])))
        own = jnp.concatenate([tokens, meta], axis=1)

        low, high = lax.optimization_barrier((line_move(own, 1), line_move(own, -1)))
        near = jnp.concatenate([low, own, high], axis=0)
        far_low = line_move(near, reach - 1)
        far_high = line_move(near[count:], 2 - reach)
        far = jnp.concatenate(lax.optimization_barrier((far_low, far_high)), axis=0)

        swap = [(c, cores - 1 - c) for c in range(cores)]
        pair = [lax.ppermute(w, "core", swap) for w in (w_gate, w_up, w_down)]
        weights = [
            pltpu.with_memory_space_constraint(w, pltpu.VMEM) for w in (w_gate, w_up)
        ] + [
            pltpu.with_memory_space_constraint(w, pltpu.HBM) for w in (*pair[:2], w_down, pair[2])
        ]

        right, left = [near, far], [near, far]
        got = [{0: right[0]}, {0: right[1]}]
        for k in range(1, reach + 1):
            for c in range(2):
                if k < reach:
                    pair = ring_move(right[c], 1), ring_move(left[c], -1)
                    right[c], left[c] = lax.optimization_barrier(pair)
                    got[c][-k], got[c][k] = right[c], left[c]
                else:
                    got[c][k] = ring_move(right[c], 1) if c == 0 else ring_move(left[c], -1)

        outs = [{}, {}]
        for offsets in ((0, -1, 1), (-2, 2), (-3, 3, reach)):
            where = [(c, d) for d in offsets for c in range(2)]
            parts = experts(node, [got[c][d] for c, d in where], weights, top, count)
            for (c, d), part in zip(where, parts):
                outs[c][d] = part

        to_left, to_right, sums = [None, None], [None, None], []
        for k in range(reach, 0, -1):
            for c in (1, 0):
                out = outs[c]
                if k == reach:
                    moved = ring_move(out[k], -1 if c == 0 else 1)
                    (to_left if c == 0 else to_right)[c] = moved
                else:
                    go_left = out[-k] if to_left[c] is None else add(out[-k], to_left[c])
                    go_right = out[k] if to_right[c] is None else add(out[k], to_right[c])
                    go_left, go_right = lax.optimization_barrier((go_left, go_right))
                    to_left[c], to_right[c] = ring_move(go_left, -1), ring_move(go_right, 1)
        for c in range(2):
            value = add(add(outs[c][0].astype(jnp.float32), to_left[c]), to_right[c])
            sums.append(value if c == 0 else value.astype(tokens.dtype))

        near, far = sums
        triple = line_move(far[: 3 * count], 1 - reach)
        double = line_move(far[3 * count :], reach - 2)
        near = near + triple.astype(jnp.float32)
        double = double.astype(jnp.float32)
        total = near[count : 2 * count] + double[:count]
        low = near[:count].astype(tokens.dtype)
        high = (near[2 * count :] + double[count:]).astype(tokens.dtype)
        low, high = line_move(low, -1), line_move(high, 1)
        total = total + low.astype(jnp.float32) + high.astype(jnp.float32)
        return total.astype(tokens.dtype)

    return local


def solution(mesh):
    parts, nodes, shares = mesh.devices.shape
    cores = 2
    chips = shares // cores
    plane = Mesh(
        mesh.devices.reshape(parts, nodes, chips, cores), ("parts", "node", "chip", "core")
    )
    token_spec = P(("parts", "node", "chip", "core"), None)
    in_specs = (
        token_spec,
        token_spec,
        token_spec,
        token_spec,
        P(("parts", "node"), None, ("chip", "core")),
        P(("parts", "node"), None, ("chip", "core")),
        P(("parts", "node"), ("chip", "core"), None),
    )
    return jax.shard_map(
        build(nodes, chips, cores),
        mesh=plane,
        in_specs=in_specs,
        out_specs=token_spec,
        check_vma=False,
    )
```

profile of v0, /device:TPU:514, one launch (start us, length us, event | category | flops | bytes accessed | tf_op | source)
XLA Modules:
  0.0 221.8 jit_solution(472024094101444076)
XLA Ops:
  3.0 19.5 %collective-permute-start.1 = (bf16[8,7296]{1,0:T(8,128)(2,1)S(1)}, bf16[8,7296]{1,0:T(8,128)(2,1)S(1)}, u32[]{:S(2)}, u32[]{:S(2)}) collective-permute-start(bf16[8,7296]{1,0:T(8,128)(2,1)S(1)} %pad_maximum_fusion.2), channel_id=1, source_target_pairs={{0,112},{1,15},{2,114},{3,1},{4,116},{5,3},{6,118},{7,5},{8,120},{... | collective-permute-start | bytes 350216 | tf_op jit(solution)/shard_map/ppermute | solution.py:141
  29.4 3.7 %collective-permute-start.3 = (bf16[16,7296]{1,0:T(8,128)(2,1)S(1)}, bf16[16,7296]{1,0:T(8,128)(2,1)S(1)}, u32[]{:S(2)}, u32[]{:S(2)}) collective-permute-start(bf16[16,7296]{1,0:T(8,128)(2,1)S(1)} %pad_maximum_fusion.1), channel_id=1, source_target_pairs={{0,96},{1,13},{2,98},{3,15},{4,100},{5,1},{6,102},{7,3},{8,104},{9... | collective-permute-start | bytes 700424 | tf_op jit(solution)/shard_map/ppermute | solution.py:141
  33.5 6.6 %collective-permute-done.3 = bf16[16,7296]{1,0:T(8,128)(2,1)S(1)} collective-permute-done((bf16[16,7296]{1,0:T(8,128)(2,1)S(1)}, bf16[16,7296]{1,0:T(8,128)(2,1)S(1)}, u32[]{:S(2)}, u32[]{:S(2)}) %collective-permute-start.3) | collective-permute-done | bytes 233504 | tf_op jit(solution)/shard_map/ppermute | solution.py:141
  40.2 9.1 %collective-permute-done.2 = bf16[24,7296]{1,0:T(8,128)(2,1)S(1)} collective-permute-done((bf16[24,7296]{1,0:T(8,128)(2,1)S(1)}, bf16[24,7296]{1,0:T(8,128)(2,1)S(1)}, u32[]{:S(2)}, u32[]{:S(2)}) %collective-permute-start.2) | collective-permute-done | bytes 350240 | tf_op jit(solution)/shard_map/ppermute | solution.py:141
  51.4 7.8 %collective-permute-done.7.refs_5_ = bf16[40,7296]{1,0:T(8,128)(2,1)S(1)} collective-permute-done((bf16[40,7296]{1,0:T(8,128)(2,1)S(1)}, bf16[40,7296]{1,0:T(8,128)(2,1)S(1)}, u32[]{:S(2)}, u32[]{:S(2)}) %collective-permute-start.7) | collective-permute-done | bytes 583712 | tf_op jit(solution)/shard_map/ppermute | solution.py:138
  61.2 5.3 %collective-permute-done.5.refs_4_ = bf16[24,7296]{1,0:T(8,128)(2,1)S(1)} collective-permute-done((bf16[24,7296]{1,0:T(8,128)(2,1)S(1)}, bf16[24,7296]{1,0:T(8,128)(2,1)S(1)}, u32[]{:S(2)}, u32[]{:S(2)}) %collective-permute-start.5) | collective-permute-done | bytes 350240 | tf_op jit(solution)/shard_map/ppermute | solution.py:138
  69.8 7.8 %collective-permute-done.13.refs_1_ = bf16[40,7296]{1,0:T(8,128)(2,1)S(1)} collective-permute-done((bf16[40,7296]{1,0:T(8,128)(2,1)S(1)}, bf16[40,7296]{1,0:T(8,128)(2,1)S(1)}, u32[]{:S(2)}, u32[]{:S(2)}) %collective-permute-start.13) | collective-permute-done | bytes 583712 | tf_op jit(solution)/shard_map/ppermute | solution.py:138
  82.3 3.8 %collective-permute-done.11.refs_0_ = bf16[24,7296]{1,0:T(8,128)(2,1)S(1)} collective-permute-done((bf16[24,7296]{1,0:T(8,128)(2,1)S(1)}, bf16[24,7296]{1,0:T(8,128)(2,1)S(1)}, u32[]{:S(2)}, u32[]{:S(2)}) %collective-permute-start.11) | collective-permute-done | bytes 350240 | tf_op jit(solution)/shard_map/ppermute | solution.py:138
  86.4 3.7 %collective-permute-start.18 = (bf16[40,7296]{1,0:T(8,128)(2,1)S(1)}, bf16[40,7296]{1,0:T(8,128)(2,1)}, u32[]{:S(2)}, u32[]{:S(2)}) collective-permute-start(bf16[40,7296]{1,0:T(8,128)(2,1)S(1)} %collective-permute-done.14.refs_3_), channel_id=1, source_target_pairs={{0,14},{1,113},{2,0},{3,115},{4,2},{5,117},{6,4},{7,119},{8,6},{9,... | collective-permute-start | bytes 1751048 | tf_op jit(solution)/shard_map/ppermute | solution.py:138
  90.1 7.1 %collective-permute-done.17.refs_1_ = bf16[40,7296]{1,0:T(8,128)(2,1)S(1)} collective-permute-done((bf16[40,7296]{1,0:T(8,128)(2,1)S(1)}, bf16[40,7296]{1,0:T(8,128)(2,1)S(1)}, u32[]{:S(2)}, u32[]{:S(2)}) %collective-permute-start.17) | collective-permute-done | bytes 583712 | tf_op jit(solution)/shard_map/ppermute | solution.py:138
  102.7 3.9 %collective-permute-done.15.refs_0_ = bf16[24,7296]{1,0:T(8,128)(2,1)} collective-permute-done((bf16[24,7296]{1,0:T(8,128)(2,1)S(1)}, bf16[24,7296]{1,0:T(8,128)(2,1)}, u32[]{:S(2)}, u32[]{:S(2)}) %collective-permute-start.15) | collective-permute-done | bytes 350240 | tf_op jit(solution)/shard_map/ppermute | solution.py:138
  109.4 7.4 %collective-permute-done.19.refs_4_ = bf16[24,7296]{1,0:T(8,128)(2,1)} collective-permute-done((bf16[24,7296]{1,0:T(8,128)(2,1)}, bf16[24,7296]{1,0:T(8,128)(2,1)}, u32[]{:S(2)}, u32[]{:S(2)}) %collective-permute-start.19) | collective-permute-done | bytes 350240 | tf_op jit(solution)/shard_map/ppermute | solution.py:138
  123.0 10.6 %experts.5 = (bf16[24,7168]{1,0:T(8,128)(2,1)S(1)}, bf16[40,7168]{1,0:T(8,128)(2,1)S(1)}, bf16[24,7168]{1,0:T(8,128)(2,1)S(1)}, bf16[40,7168]{1,0:T(8,128)(2,1)S...) custom-call(s32[1]{0:T(128)} %bitcast.node_ref, bf16[24,7296]{1,0:T(8,128)(2,1)} %collective-permute-done.15.refs_0_, ...), custom_call_target="tpu_custom_call" | custom-call | flops 4227858432 | bytes 5505024 | tf_op jit(solution)/shard_map/experts/pallas_call | solution.py:113
  135.8 7.5 %experts.4 = (bf16[24,7168]{1,0:T(8,128)(2,1)S(1)}, bf16[40,7168]{1,0:T(8,128)(2,1)S(1)}, bf16[24,7168]{1,0:T(8,128)(2,1)S(1)}, bf16[40,7168]{1,0:T(8,128)(2,1)S(1)}) custom-call(s32[1]{0:T(128)} %bitcast.node_ref, bf16[24,7296]{1,0:T(8,128)(2,1)S(1)} %copy-done.11, bf16[40,7296]{1,0:T(8,128)(2,1)S(1)} %collective-permute-done.13.refs_1_, ...), custom_call_target="tpu_custom_call" | custom-call | flops 2818572288 | bytes 3670016 | tf_op jit(solution)/shard_map/experts/pallas_call | solution.py:113
  143.4 8.3 %experts.3 = (bf16[24,7168]{1,0:T(8,128)(2,1)S(1)}, bf16[40,7168]{1,0:T(8,128)(2,1)S(1)}, bf16[24,7168]{1,0:T(8,128)(2,1)S(1)}, bf16[40,7168]{1,0:T(8,128)(2,1)S...) custom-call(s32[1]{0:T(128)} %bitcast.node_ref, bf16[24,7296]{1,0:T(8,128)(2,1)S(1)} %pad_maximum_fusion.refs_0_, ...), custom_call_target="tpu_custom_call" | custom-call | flops 4227858432 | bytes 5505024 | tf_op jit(solution)/shard_map/experts/pallas_call | solution.py:113
  155.2 3.3 %collective-permute-start.29 = (bf16[40,7168]{1,0:T(8,128)(2,1)S(1)}, bf16[40,7168]{1,0:T(8,128)(2,1)S(1)}, u32[]{:S(2)}, u32[]{:S(2)}) collective-permute-start(bf16[40,7168]{1,0:T(8,128)(2,1)S(1)} %get-tuple-element.85), channel_id=1, source_target_pairs={{0,14},{1,113},{2,0},{3,115},{4,2},{5,117},{6,4},{7,119},{8,6},{9,... | collective-permute-start | bytes 1720328 | tf_op jit(solution)/shard_map/ppermute | solution.py:138
  159.9 3.6 %collective-permute-done.23 = bf16[24,7168]{1,0:T(8,128)(2,1)S(1)} collective-permute-done((bf16[24,7168]{1,0:T(8,128)(2,1)S(1)}, bf16[24,7168]{1,0:T(8,128)(2,1)S(1)}, u32[]{:S(2)}, u32[]{:S(2)}) %collective-permute-start.23) | collective-permute-done | bytes 344096 | tf_op jit(solution)/shard_map/ppermute | solution.py:138
  166.1 3.6 %collective-permute-done.30 = bf16[40,7168]{1,0:T(8,128)(2,1)S(1)} collective-permute-done((bf16[40,7168]{1,0:T(8,128)(2,1)S(1)}, bf16[40,7168]{1,0:T(8,128)(2,1)S(1)}, u32[]{:S(2)}, u32[]{:S(2)}) %collective-permute-start.30) | collective-permute-done | bytes 573472 | tf_op jit(solution)/shard_map/ppermute | solution.py:138
  172.1 16.0 %collective-permute-done.31 = bf16[40,7168]{1,0:T(8,128)(2,1)S(1)} collective-permute-done((bf16[40,7168]{1,0:T(8,128)(2,1)S(1)}, bf16[40,7168]{1,0:T(8,128)(2,1)S(1)}, u32[]{:S(2)}, u32[]{:S(2)}) %collective-permute-start.31) | collective-permute-done | bytes 573472 | tf_op jit(solution)/shard_map/ppermute | solution.py:138
  191.3 3.3 %collective-permute-start.26 = (bf16[24,7168]{1,0:T(8,128)(2,1)S(1)}, bf16[24,7168]{1,0:T(8,128)(2,1)S(1)}, u32[]{:S(2)}, u32[]{:S(2)}) collective-permute-start(bf16[24,7168]{1,0:T(8,128)(2,1)S(1)} %add_convert_fusion.7), channel_id=1, source_target_pairs={{0,14},{1,113},{2,0},{3,115},{4,2},{5,117},{6,4},{7,119},{8,6},{9,... | collective-permute-start | bytes 1032200 | tf_op jit(solution)/shard_map/ppermute | solution.py:138
  194.7 4.4 %collective-permute-done.33 = bf16[40,7168]{1,0:T(8,128)(2,1)S(1)} collective-permute-done((bf16[40,7168]{1,0:T(8,128)(2,1)S(1)}, bf16[40,7168]{1,0:T(8,128)(2,1)S(1)}, u32[]{:S(2)}, u32[]{:S(2)}) %collective-permute-start.33) | collective-permute-done | bytes 573472 | tf_op jit(solution)/shard_map/ppermute | solution.py:138
  199.0 3.4 %collective-permute-done.34 = bf16[40,7168]{1,0:T(8,128)(2,1)S(1)} collective-permute-done((bf16[40,7168]{1,0:T(8,128)(2,1)S(1)}, bf16[40,7168]{1,0:T(8,128)(2,1)S(1)}, u32[]{:S(2)}, u32[]{:S(2)}) %collective-permute-start.34) | collective-permute-done | bytes 573472 | tf_op jit(solution)/shard_map/ppermute | solution.py:138
  203.0 8.7 %collective-permute-done.36 = bf16[16,7168]{1,0:T(8,128)(2,1)S(1)} collective-permute-done((bf16[16,7168]{1,0:T(8,128)(2,1)S(1)}, bf16[16,7168]{1,0:T(8,128)(2,1)S(1)}, u32[]{:S(2)}, u32[]{:S(2)}) %collective-permute-start.36) | collective-permute-done | bytes 229408 | tf_op jit(solution)/shard_map/ppermute | solution.py:141
  211.7 4.1 %collective-permute-done.35 = bf16[24,7168]{1,0:T(8,128)(2,1)S(1)} collective-permute-done((bf16[24,7168]{1,0:T(8,128)(2,1)S(1)}, bf16[24,7168]{1,0:T(8,128)(2,1)S(1)}, u32[]{:S(2)}, u32[]{:S(2)}) %collective-permute-start.35) | collective-permute-done | bytes 344096 | tf_op jit(solution)/shard_map/ppermute | solution.py:141
  (115 shorter events, 58.9 us)
Async XLA Ops:
  3.0 21.9 %collective-permute-start.1 = (bf16[8,7296]{1,0:T(8,128)(2,1)S(1)}, bf16[8,7296]{1,0:T(8,128)(2,1)S(1)}, u32[]{:S(2)}, u32[]{:S(2)}) collective-permute-start(bf16[8,7296]{1,0:T(8,128)(2,1)S(1)} %pad_maximum_fusion.2), channel_id=1, source_target_pairs={{0,112},{1,15},{2,114},{3,1},{4,116},{5,3},{6,118},{7,5},{8,120},{... | collective-permute-start | bytes 350216 | tf_op jit(solution)/shard_map/ppermute | solution.py:141
  28.3 20.9 %collective-permute-start.2 = (bf16[24,7296]{1,0:T(8,128)(2,1)S(1)}, bf16[24,7296]{1,0:T(8,128)(2,1)S(1)}, u32[]{:S(2)}, u32[]{:S(2)}) collective-permute-start(bf16[24,7296]{1,0:T(8,128)(2,1)S(1)} %pad_maximum_fusion.refs_0_), channel_id=1, source_target_pairs={{0,48},{1,7},{2,50},{3,9},{4,52},{5,11},{6,54},{7,13},{8,56},{9,15... | collective-permute-start | bytes 1050632 | tf_op jit(solution)/shard_map/ppermute | solution.py:141
  29.4 10.8 %collective-permute-start.3 = (bf16[16,7296]{1,0:T(8,128)(2,1)S(1)}, bf16[16,7296]{1,0:T(8,128)(2,1)S(1)}, u32[]{:S(2)}, u32[]{:S(2)}) collective-permute-start(bf16[16,7296]{1,0:T(8,128)(2,1)S(1)} %pad_maximum_fusion.1), channel_id=1, source_target_pairs={{0,96},{1,13},{2,98},{3,15},{4,100},{5,1},{6,102},{7,3},{8,104},{9... | collective-permute-start | bytes 700424 | tf_op jit(solution)/shard_map/ppermute | solution.py:141
  33.0 83.8 %collective-permute-start.8 = (bf16[2,7168,128]{2,1,0:T(8,128)(2,1)}, bf16[2,7168,128]{2,1,0:T(8,128)(2,1)}, u32[]{:S(2)}, u32[]{:S(2)}) collective-permute-start(bf16[2,7168,128]{2,1,0:T(8,128)(2,1)} %refs_6_.3), channel_id=1, source_target_pairs={{0,1},{1,0},{2,3},{3,2},{4,5},{5,4},{6,7},{7,6},{8,9},{9,8},{10,11... | collective-permute-start | bytes 11010056 | tf_op jit(solution)/shard_map/ppermute | solution.py:162
  33.0 83.8 %collective-permute-start.9 = (bf16[2,7168,128]{2,1,0:T(8,128)(2,1)}, bf16[2,7168,128]{2,1,0:T(8,128)(2,1)}, u32[]{:S(2)}, u32[]{:S(2)}) collective-permute-start(bf16[2,7168,128]{2,1,0:T(8,128)(2,1)} %refs_7_.3), channel_id=1, source_target_pairs={{0,1},{1,0},{2,3},{3,2},{4,5},{5,4},{6,7},{7,6},{8,9},{9,8},{10,11... | collective-permute-start | bytes 11010056 | tf_op jit(solution)/shard_map/ppermute | solution.py:162
  33.5 83.3 %collective-permute-start.10 = (bf16[2,128,7168]{2,1,0:T(8,128)(2,1)}, bf16[2,128,7168]{2,1,0:T(8,128)(2,1)}, u32[]{:S(2)}, u32[]{:S(2)}) collective-permute-start(bf16[2,128,7168]{2,1,0:T(8,128)(2,1)} %refs_10_.3), channel_id=1, source_target_pairs={{0,1},{1,0},{2,3},{3,2},{4,5},{5,4},{6,7},{7,6},{8,9},{9,8},{10,11... | collective-permute-start | bytes 11010056 | tf_op jit(solution)/shard_map/ppermute | solution.py:162
  49.3 9.9 %collective-permute-start.7 = (bf16[40,7296]{1,0:T(8,128)(2,1)S(1)}, bf16[40,7296]{1,0:T(8,128)(2,1)S(1)}, u32[]{:S(2)}, u32[]{:S(2)}) collective-permute-start(bf16[40,7296]{1,0:T(8,128)(2,1)S(1)} %constant_dynamic-update-slice_fusion.refs_1_), channel_id=1, source_target_pairs={{0,14},{1,113},{2,0},{3,115},{4,2},{5,117},{6,4},{7,119},{8,6},{9,... | collective-permute-start | bytes 1751048 | tf_op jit(solution)/shard_map/ppermute | solution.py:138
  49.4 11.1 %collective-permute-start.6 = (bf16[40,7296]{1,0:T(8,128)(2,1)S(1)}, bf16[40,7296]{1,0:T(8,128)(2,1)S(1)}, u32[]{:S(2)}, u32[]{:S(2)}) collective-permute-start(bf16[40,7296]{1,0:T(8,128)(2,1)S(1)} %constant_dynamic-update-slice_fusion.refs_1_), channel_id=1, source_target_pairs={{0,2},{1,17},{2,4},{3,19},{4,6},{5,21},{6,8},{7,23},{8,10},{9,25},... | collective-permute-start | bytes 1751048 | tf_op jit(solution)/shard_map/ppermute | solution.py:138
  66.5 11.0 %collective-permute-start.13 = (bf16[40,7296]{1,0:T(8,128)(2,1)S(1)}, bf16[40,7296]{1,0:T(8,128)(2,1)S(1)}, u32[]{:S(2)}, u32[]{:S(2)}) collective-permute-start(bf16[40,7296]{1,0:T(8,128)(2,1)S(1)} %collective-permute-done.6.refs_3_), channel_id=1, source_target_pairs={{0,2},{1,17},{2,4},{3,19},{4,6},{5,21},{6,8},{7,23},{8,10},{9,25},... | collective-permute-start | bytes 1751048 | tf_op jit(solution)/shard_map/ppermute | solution.py:138
  86.1 11.0 %collective-permute-start.17 = (bf16[40,7296]{1,0:T(8,128)(2,1)S(1)}, bf16[40,7296]{1,0:T(8,128)(2,1)S(1)}, u32[]{:S(2)}, u32[]{:S(2)}) collective-permute-start(bf16[40,7296]{1,0:T(8,128)(2,1)S(1)} %collective-permute-done.13.refs_1_), channel_id=1, source_target_pairs={{0,2},{1,17},{2,4},{3,19},{4,6},{5,21},{6,8},{7,23},{8,10},{9,25},... | collective-permute-start | bytes 1751048 | tf_op jit(solution)/shard_map/ppermute | solution.py:138
  86.4 12.3 %collective-permute-start.18 = (bf16[40,7296]{1,0:T(8,128)(2,1)S(1)}, bf16[40,7296]{1,0:T(8,128)(2,1)}, u32[]{:S(2)}, u32[]{:S(2)}) collective-permute-start(bf16[40,7296]{1,0:T(8,128)(2,1)S(1)} %collective-permute-done.14.refs_3_), channel_id=1, source_target_pairs={{0,14},{1,113},{2,0},{3,115},{4,2},{5,117},{6,4},{7,119},{8,6},{9,... | collective-permute-start | bytes 1751048 | tf_op jit(solution)/shard_map/ppermute | solution.py:138
  106.6 10.2 %collective-permute-start.20 = (bf16[40,7296]{1,0:T(8,128)(2,1)}, bf16[40,7296]{1,0:T(8,128)(2,1)}, u32[]{:S(2)}, u32[]{:S(2)}) collective-permute-start(bf16[40,7296]{1,0:T(8,128)(2,1)} %collective-permute-done.18.refs_3_), channel_id=1, source_target_pairs={{0,14},{1,113},{2,0},{3,115},{4,2},{5,117},{6,4},{7,119},{8,6},{9,... | collective-permute-start | bytes 1751048 | tf_op jit(solution)/shard_map/ppermute | solution.py:138
  133.6 18.0 %collective-permute-start.21 = (bf16[24,7168]{1,0:T(8,128)(2,1)S(1)}, bf16[24,7168]{1,0:T(8,128)(2,1)S(1)}, u32[]{:S(2)}, u32[]{:S(2)}) collective-permute-start(bf16[24,7168]{1,0:T(8,128)(2,1)S(1)} %get-tuple-element.69), channel_id=1, source_target_pairs={{0,14},{1,113},{2,0},{3,115},{4,2},{5,117},{6,4},{7,119},{8,6},{9,... | collective-permute-start | bytes 1032200 | tf_op jit(solution)/shard_map/ppermute | solution.py:138
  135.7 19.3 %collective-permute-start.28 = (bf16[40,7168]{1,0:T(8,128)(2,1)S(1)}, bf16[40,7168]{1,0:T(8,128)(2,1)S(1)}, u32[]{:S(2)}, u32[]{:S(2)}) collective-permute-start(bf16[40,7168]{1,0:T(8,128)(2,1)S(1)} %get-tuple-element.84), channel_id=1, source_target_pairs={{0,2},{1,17},{2,4},{3,19},{4,6},{5,21},{6,8},{7,23},{8,10},{9,25},... | collective-permute-start | bytes 1720328 | tf_op jit(solution)/shard_map/ppermute | solution.py:138
  155.2 10.8 %collective-permute-start.29 = (bf16[40,7168]{1,0:T(8,128)(2,1)S(1)}, bf16[40,7168]{1,0:T(8,128)(2,1)S(1)}, u32[]{:S(2)}, u32[]{:S(2)}) collective-permute-start(bf16[40,7168]{1,0:T(8,128)(2,1)S(1)} %get-tuple-element.85), channel_id=1, source_target_pairs={{0,14},{1,113},{2,0},{3,115},{4,2},{5,117},{6,4},{7,119},{8,6},{9,... | collective-permute-start | bytes 1720328 | tf_op jit(solution)/shard_map/ppermute | solution.py:138
  158.5 11.1 %collective-permute-start.30 = (bf16[40,7168]{1,0:T(8,128)(2,1)S(1)}, bf16[40,7168]{1,0:T(8,128)(2,1)S(1)}, u32[]{:S(2)}, u32[]{:S(2)}) collective-permute-start(bf16[40,7168]{1,0:T(8,128)(2,1)S(1)} %add_convert_fusion.5), channel_id=1, source_target_pairs={{0,2},{1,17},{2,4},{3,19},{4,6},{5,21},{6,8},{7,23},{8,10},{9,25},... | collective-permute-start | bytes 1720328 | tf_op jit(solution)/shard_map/ppermute | solution.py:138
  163.8 27.4 %collective-permute-start.25 = (bf16[24,7168]{1,0:T(8,128)(2,1)S(1)}, bf16[24,7168]{1,0:T(8,128)(2,1)S(1)}, u32[]{:S(2)}, u32[]{:S(2)}) collective-permute-start(bf16[24,7168]{1,0:T(8,128)(2,1)S(1)} %add_convert_fusion.8), channel_id=1, source_target_pairs={{0,2},{1,17},{2,4},{3,19},{4,6},{5,21},{6,8},{7,23},{8,10},{9,25},... | collective-permute-start | bytes 1032200 | tf_op jit(solution)/shard_map/ppermute | solution.py:138
  169.8 18.4 %collective-permute-start.31 = (bf16[40,7168]{1,0:T(8,128)(2,1)S(1)}, bf16[40,7168]{1,0:T(8,128)(2,1)S(1)}, u32[]{:S(2)}, u32[]{:S(2)}) collective-permute-start(bf16[40,7168]{1,0:T(8,128)(2,1)S(1)} %add_convert_fusion.4), channel_id=1, source_target_pairs={{0,14},{1,113},{2,0},{3,115},{4,2},{5,117},{6,4},{7,119},{8,6},{9,... | collective-permute-start | bytes 1720328 | tf_op jit(solution)/shard_map/ppermute | solution.py:138
  171.0 17.3 %collective-permute-start.32 = (bf16[40,7168]{1,0:T(8,128)(2,1)S(1)}, bf16[40,7168]{1,0:T(8,128)(2,1)S(1)}, u32[]{:S(2)}, u32[]{:S(2)}) collective-permute-start(bf16[40,7168]{1,0:T(8,128)(2,1)S(1)} %add_convert_fusion.3), channel_id=1, source_target_pairs={{0,2},{1,17},{2,4},{3,19},{4,6},{5,21},{6,8},{7,23},{8,10},{9,25},... | collective-permute-start | bytes 1720328 | tf_op jit(solution)/shard_map/ppermute | solution.py:138
  188.4 10.6 %collective-permute-start.33 = (bf16[40,7168]{1,0:T(8,128)(2,1)S(1)}, bf16[40,7168]{1,0:T(8,128)(2,1)S(1)}, u32[]{:S(2)}, u32[]{:S(2)}) collective-permute-start(bf16[40,7168]{1,0:T(8,128)(2,1)S(1)} %add_convert_fusion.2), channel_id=1, source_target_pairs={{0,14},{1,113},{2,0},{3,115},{4,2},{5,117},{6,4},{7,119},{8,6},{9,... | collective-permute-start | bytes 1720328 | tf_op jit(solution)/shard_map/ppermute | solution.py:138
  191.2 11.2 %collective-permute-start.34 = (bf16[40,7168]{1,0:T(8,128)(2,1)S(1)}, bf16[40,7168]{1,0:T(8,128)(2,1)S(1)}, u32[]{:S(2)}, u32[]{:S(2)}) collective-permute-start(bf16[40,7168]{1,0:T(8,128)(2,1)S(1)} %add_convert_fusion.1), channel_id=1, source_target_pairs={{0,2},{1,17},{2,4},{3,19},{4,6},{5,21},{6,8},{7,23},{8,10},{9,25},... | collective-permute-start | bytes 1720328 | tf_op jit(solution)/shard_map/ppermute | solution.py:138
  191.3 20.4 %collective-permute-start.26 = (bf16[24,7168]{1,0:T(8,128)(2,1)S(1)}, bf16[24,7168]{1,0:T(8,128)(2,1)S(1)}, u32[]{:S(2)}, u32[]{:S(2)}) collective-permute-start(bf16[24,7168]{1,0:T(8,128)(2,1)S(1)} %add_convert_fusion.7), channel_id=1, source_target_pairs={{0,14},{1,113},{2,0},{3,115},{4,2},{5,117},{6,4},{7,119},{8,6},{9,... | collective-permute-start | bytes 1032200 | tf_op jit(solution)/shard_map/ppermute | solution.py:138
  194.7 17.1 %collective-permute-start.27 = (bf16[24,7168]{1,0:T(8,128)(2,1)S(1)}, bf16[24,7168]{1,0:T(8,128)(2,1)S(1)}, u32[]{:S(2)}, u32[]{:S(2)}) collective-permute-start(bf16[24,7168]{1,0:T(8,128)(2,1)S(1)} %add_convert_fusion.6), channel_id=1, source_target_pairs={{0,2},{1,17},{2,4},{3,19},{4,6},{5,21},{6,8},{7,23},{8,10},{9,25},... | collective-permute-start | bytes 1032200 | tf_op jit(solution)/shard_map/ppermute | solution.py:138
  202.7 13.1 %collective-permute-start.35 = (bf16[24,7168]{1,0:T(8,128)(2,1)S(1)}, bf16[24,7168]{1,0:T(8,128)(2,1)S(1)}, u32[]{:S(2)}, u32[]{:S(2)}) collective-permute-start(bf16[24,7168]{1,0:T(8,128)(2,1)S(1)} %slice.31), channel_id=1, source_target_pairs={{0,80},{1,11},{2,82},{3,13},{4,84},{5,15},{6,86},{7,1},{8,88},{9,3... | collective-permute-start | bytes 1032200 | tf_op jit(solution)/shard_map/ppermute | solution.py:141
  (31 other events, 192.1 us)
where the time goes:
time: 222 us
  waiting for transfers between devices  116 us (52%)
  starting transfers between devices  60.7 us (27%)
  Pallas kernels  26.5 us (12%)
  local copies, waits for them, and re-layouts  10.8 us (5%)
  other arithmetic  7.13 us (3%)
    ppermute x28, waiting for transfers between devices, ring_move(): return lax.ppermute(x, PLANE, shift_pairs(nodes, chips, cores, True, step))  80.2 us
    ppermute x8, waiting for transfers between devices, line_move(): return lax.ppermute(x, PLANE, shift_pairs(nodes, chips, cores, False, step))  36.2 us
    ppermute x28, starting transfers between devices, ring_move(): return lax.ppermute(x, PLANE, shift_pairs(nodes, chips, cores, True, step))  34.5 us
    pallas_call x3, Pallas kernels, experts(): pl.pallas_call(functools.partial(expert_kernel, len(pieces), width, top,...  26.5 us
    ppermute x8, starting transfers between devices, line_move(): return lax.ppermute(x, PLANE, shift_pairs(nodes, chips, cores, False, step))  25.7 us
    unnamed x33, local copies, waits for them, and re-layouts  10.7 us
  transfers between devices with their start and end apart: 39, of which 28 were waited for; matrix products, arithmetic and copies ran while one was open for 1% of the time, Pallas kernels for 7%

commit v1 on v0

--- a/solution.py
+++ b/solution.py
@@ -28,7 +28,7 @@
     return pairs
 
 
-def expert_kernel(pieces, width, top, count, steps, steps_out, node_ref, *refs):
+def expert_kernel(pieces, width, top, first, count, steps, steps_out, node_ref, *refs):
     x_refs, refs = refs[:pieces], refs[pieces:]
     w_gate, w_up, p_gate, p_up, w_down, p_down = refs[:6]
     out_refs, (acc, hid, *held, sems) = refs[6 : 6 + pieces], refs[6 + pieces :]
@@ -61,9 +61,9 @@
     meta = jnp.concatenate([r[:, width : width + LANES] for r in x_refs], axis=0)
     meta = meta.astype(jnp.float32)
     lane = lax.broadcasted_iota(jnp.int32, meta.shape, 1)
-    weights = pltpu.roll(meta, LANES - top, 1)
+    weights = pltpu.roll(meta, LANES - first, 1)
     node = node_ref[0]
-    slot = jnp.sum(jnp.where(lane == 2 * top + node, meta, 0.0), axis=1, keepdims=True)
+    slot = jnp.sum(jnp.where(lane == top + node, meta, 0.0), axis=1, keepdims=True)
     reached = jnp.where(slot < count, 1.0, 0.0)
     gates = []
     for m in range(per_node):
@@ -102,7 +102,7 @@
             o[:, at] = y[ends[j] : ends[j + 1]].astype(o.dtype)
 
 
-def experts(node, pieces, weights, top, count):
+def experts(node, pieces, weights, top, first, count):
     per_node, width, units = weights[0].shape
     lanes = per_node * units
     steps = next(n for n in (4, 7, 1) if width % (n * LANES) == 0)
@@ -111,7 +111,7 @@
     vmem = pl.BlockSpec(memory_space=pltpu.VMEM)
     hbm = pl.BlockSpec(memory_space=pltpu.HBM)
     return pl.pallas_call(
-        functools.partial(expert_kernel, len(pieces), width, top, count, steps, steps_out),
+        functools.partial(expert_kernel, len(pieces), width, top, first, count, steps, steps_out),
         out_shape=[jax.ShapeDtypeStruct((p.shape[0], width), p.dtype) for p in pieces],
         in_specs=[pl.BlockSpec(memory_space=pltpu.SMEM)] + [vmem] * (len(pieces) + 2) + [hbm] * 4,
         out_specs=[vmem] * len(pieces),
@@ -148,7 +148,8 @@
         top = expert_ids.shape[1]
         node = lax.axis_index("node").astype(jnp.int32).reshape(1)
 
-        meta = jnp.concatenate([a.astype(tokens.dtype) for a in (expert_ids, gate_weights, slots)], 1)
+        marks = jnp.concatenate([expert_ids, slots], axis=1).astype(tokens.dtype)
+        meta = jnp.concatenate([marks, gate_weights], axis=1)
         meta = jnp.pad(meta, ((0, 0), (0, LANES - meta.shape[1])))
         own = jnp.concatenate([tokens, meta], axis=1)
 
@@ -178,9 +179,9 @@
                     got[c][k] = ring_move(right[c], 1) if c == 0 else ring_move(left[c], -1)
 
         outs = [{}, {}]
-        for offsets in ((0, -1, 1), (-2, 2), (-3, 3, reach)):
+        for offsets in ((0, -1, 1), (-2, 2, -3, 3, reach)):
             where = [(c, d) for d in offsets for c in range(2)]
-            parts = experts(node, [got[c][d] for c, d in where], weights, top, count)
+            parts = experts(node, [got[c][d] for c, d in where], weights, top, marks.shape[1], count)
             for (c, d), part in zip(where, parts):
                 outs[c][d] = part
 

time: 222 us -> 219 us (0.986)
  Pallas kernels: 26.5 us -> 20.8 us
    pallas_call x3 -> x2, Pallas kernels: 26.5 us -> 20.8 us  [experts(): pl.pallas_call(functools.partial(expert_kernel, len(pieces), width, top,...]
  transfers between devices with their start and end apart: 39 -> 39, of which waited for: 28 -> 28; matrix products, arithmetic and copies ran while one was open for 1% -> 1% of each run, Pallas kernels for 7% -> 4%
where the time goes in v1:
time: 219 us; the launch traced here: 218 us
  waiting for transfers between devices  116 us (53%)
  starting transfers between devices  60.8 us (28%)
  Pallas kernels  20.8 us (9%)
  local copies, waits for them, and re-layouts  12.7 us (6%)
  other arithmetic  7.1 us (3%)
    ppermute x28, waiting for transfers between devices, ring_move(): return lax.ppermute(x, PLANE, shift_pairs(nodes, chips, cores, True, step))  80.2 us
    ppermute x8, waiting for transfers between devices, line_move(): return lax.ppermute(x, PLANE, shift_pairs(nodes, chips, cores, False, step))  36.2 us
    ppermute x28, starting transfers between devices, ring_move(): return lax.ppermute(x, PLANE, shift_pairs(nodes, chips, cores, True, step))  34.6 us
    ppermute x8, starting transfers between devices, line_move(): return lax.ppermute(x, PLANE, shift_pairs(nodes, chips, cores, False, step))  25.7 us
    pallas_call x2, Pallas kernels, experts(): pl.pallas_call(functools.partial(expert_kernel, len(pieces), width, top,...  20.8 us
    unnamed x33, local copies, waits for them, and re-layouts  12.7 us
  transfers between devices with their start and end apart: 39, of which 28 were waited for; matrix products, arithmetic and copies ran while one was open for 1% of the time, Pallas kernels for 4%

profile of v1, /device:TPU:514, one launch (start us, length us, event | category | flops | bytes accessed | tf_op | source)
XLA Modules:
  0.0 218.0 jit_solution(11343497937291015842)
XLA Ops:
  3.0 19.5 %collective-permute-start.1 = (bf16[8,7296]{1,0:T(8,128)(2,1)S(1)}, bf16[8,7296]{1,0:T(8,128)(2,1)S(1)}, u32[]{:S(2)}, u32[]{:S(2)}) collective-permute-start(bf16[8,7296]{1,0:T(8,128)(2,1)S(1)} %pad_maximum_fusion.2), channel_id=1, source_target_pairs={{0,112},{1,15},{2,114},{3,1},{4,116},{5,3},{6,118},{7,5},{8,120},{... | collective-permute-start | bytes 350216 | tf_op jit(solution)/shard_map/ppermute | solution.py:141
  29.4 3.7 %collective-permute-start.3 = (bf16[16,7296]{1,0:T(8,128)(2,1)S(1)}, bf16[16,7296]{1,0:T(8,128)(2,1)S(1)}, u32[]{:S(2)}, u32[]{:S(2)}) collective-permute-start(bf16[16,7296]{1,0:T(8,128)(2,1)S(1)} %pad_maximum_fusion.1), channel_id=1, source_target_pairs={{0,96},{1,13},{2,98},{3,15},{4,100},{5,1},{6,102},{7,3},{8,104},{9... | collective-permute-start | bytes 700424 | tf_op jit(solution)/shard_map/ppermute | solution.py:141
  33.5 6.6 %collective-permute-done.3 = bf16[16,7296]{1,0:T(8,128)(2,1)S(1)} collective-permute-done((bf16[16,7296]{1,0:T(8,128)(2,1)S(1)}, bf16[16,7296]{1,0:T(8,128)(2,1)S(1)}, u32[]{:S(2)}, u32[]{:S(2)}) %collective-permute-start.3) | collective-permute-done | bytes 233504 | tf_op jit(solution)/shard_map/ppermute | solution.py:141
  40.2 9.1 %collective-permute-done.2 = bf16[24,7296]{1,0:T(8,128)(2,1)S(1)} collective-permute-done((bf16[24,7296]{1,0:T(8,128)(2,1)S(1)}, bf16[24,7296]{1,0:T(8,128)(2,1)S(1)}, u32[]{:S(2)}, u32[]{:S(2)}) %collective-permute-start.2) | collective-permute-done | bytes 350240 | tf_op jit(solution)/shard_map/ppermute | solution.py:141
  51.4 7.8 %collective-permute-done.7.refs_5_ = bf16[40,7296]{1,0:T(8,128)(2,1)S(1)} collective-permute-done((bf16[40,7296]{1,0:T(8,128)(2,1)S(1)}, bf16[40,7296]{1,0:T(8,128)(2,1)S(1)}, u32[]{:S(2)}, u32[]{:S(2)}) %collective-permute-start.7) | collective-permute-done | bytes 583712 | tf_op jit(solution)/shard_map/ppermute | solution.py:138
  61.2 5.3 %collective-permute-done.5.refs_4_ = bf16[24,7296]{1,0:T(8,128)(2,1)S(1)} collective-permute-done((bf16[24,7296]{1,0:T(8,128)(2,1)S(1)}, bf16[24,7296]{1,0:T(8,128)(2,1)S(1)}, u32[]{:S(2)}, u32[]{:S(2)}) %collective-permute-start.5) | collective-permute-done | bytes 350240 | tf_op jit(solution)/shard_map/ppermute | solution.py:138
  69.8 7.8 %collective-permute-done.13.refs_1_ = bf16[40,7296]{1,0:T(8,128)(2,1)S(1)} collective-permute-done((bf16[40,7296]{1,0:T(8,128)(2,1)S(1)}, bf16[40,7296]{1,0:T(8,128)(2,1)S(1)}, u32[]{:S(2)}, u32[]{:S(2)}) %collective-permute-start.13) | collective-permute-done | bytes 583712 | tf_op jit(solution)/shard_map/ppermute | solution.py:138
  82.3 3.8 %collective-permute-done.11.refs_0_ = bf16[24,7296]{1,0:T(8,128)(2,1)S(1)} collective-permute-done((bf16[24,7296]{1,0:T(8,128)(2,1)S(1)}, bf16[24,7296]{1,0:T(8,128)(2,1)S(1)}, u32[]{:S(2)}, u32[]{:S(2)}) %collective-permute-start.11) | collective-permute-done | bytes 350240 | tf_op jit(solution)/shard_map/ppermute | solution.py:138
  86.4 3.7 %collective-permute-start.18 = (bf16[40,7296]{1,0:T(8,128)(2,1)S(1)}, bf16[40,7296]{1,0:T(8,128)(2,1)}, u32[]{:S(2)}, u32[]{:S(2)}) collective-permute-start(bf16[40,7296]{1,0:T(8,128)(2,1)S(1)} %collective-permute-done.14.refs_3_), channel_id=1, source_target_pairs={{0,14},{1,113},{2,0},{3,115},{4,2},{5,117},{6,4},{7,119},{8,6},{9,... | collective-permute-start | bytes 1751048 | tf_op jit(solution)/shard_map/ppermute | solution.py:138
  90.1 7.1 %collective-permute-done.17.refs_5_ = bf16[40,7296]{1,0:T(8,128)(2,1)S(1)} collective-permute-done((bf16[40,7296]{1,0:T(8,128)(2,1)S(1)}, bf16[40,7296]{1,0:T(8,128)(2,1)S(1)}, u32[]{:S(2)}, u32[]{:S(2)}) %collective-permute-start.17) | collective-permute-done | bytes 583712 | tf_op jit(solution)/shard_map/ppermute | solution.py:138
  102.7 3.9 %collective-permute-done.15.refs_4_ = bf16[24,7296]{1,0:T(8,128)(2,1)} collective-permute-done((bf16[24,7296]{1,0:T(8,128)(2,1)S(1)}, bf16[24,7296]{1,0:T(8,128)(2,1)}, u32[]{:S(2)}, u32[]{:S(2)}) %collective-permute-start.15) | collective-permute-done | bytes 350240 | tf_op jit(solution)/shard_map/ppermute | solution.py:138
  109.4 7.5 %collective-permute-done.19.refs_8_ = bf16[24,7296]{1,0:T(8,128)(2,1)} collective-permute-done((bf16[24,7296]{1,0:T(8,128)(2,1)}, bf16[24,7296]{1,0:T(8,128)(2,1)}, u32[]{:S(2)}, u32[]{:S(2)}) %collective-permute-start.19) | collective-permute-done | bytes 350240 | tf_op jit(solution)/shard_map/ppermute | solution.py:138
  124.9 12.5 %experts.3 = (bf16[24,7168]{1,0:T(8,128)(2,1)S(1)}, bf16[40,7168]{1,0:T(8,128)(2,1)S(1)}, bf16[24,7168]{1,0:T(8,128)(2,1)S(1)}, bf16[40,7168]{1,0:T(8,128)(2,1)S...) custom-call(s32[1]{0:T(128)} %bitcast.node_ref, ...), custom_call_target="tpu_custom_call" | custom-call | flops 7046430720 | bytes 9175040 | tf_op jit(solution)/shard_map/experts/pallas_call | solution.py:113
  139.6 8.3 %experts.2 = (bf16[24,7168]{1,0:T(8,128)(2,1)S(1)}, bf16[40,7168]{1,0:T(8,128)(2,1)S(1)}, bf16[24,7168]{1,0:T(8,128)(2,1)S(1)}, bf16[40,7168]{1,0:T(8,128)(2,1)S...) custom-call(s32[1]{0:T(128)} %bitcast.node_ref, bf16[24,7296]{1,0:T(8,128)(2,1)S(1)} %pad_maximum_fusion.refs_0_, ...), custom_call_target="tpu_custom_call" | custom-call | flops 4227858432 | bytes 5505024 | tf_op jit(solution)/shard_map/experts/pallas_call | solution.py:113
  148.0 3.3 %collective-permute-start.22 = (bf16[24,7168]{1,0:T(8,128)(2,1)S(1)}, bf16[24,7168]{1,0:T(8,128)(2,1)S(1)}, u32[]{:S(2)}, u32[]{:S(2)}) collective-permute-start(bf16[24,7168]{1,0:T(8,128)(2,1)S(1)} %add_convert_fusion.10), channel_id=1, source_target_pairs={{0,14},{1,113},{2,0},{3,115},{4,2},{5,117},{6,4},{7,119},{8,6},{9,... | collective-permute-start | bytes 1032200 | tf_op jit(solution)/shard_map/ppermute | solution.py:138
  151.5 3.3 %collective-permute-start.29 = (bf16[40,7168]{1,0:T(8,128)(2,1)S(1)}, bf16[40,7168]{1,0:T(8,128)(2,1)S(1)}, u32[]{:S(2)}, u32[]{:S(2)}) collective-permute-start(bf16[40,7168]{1,0:T(8,128)(2,1)S(1)} %get-tuple-element.85), channel_id=1, source_target_pairs={{0,14},{1,113},{2,0},{3,115},{4,2},{5,117},{6,4},{7,119},{8,6},{9,... | collective-permute-start | bytes 1720328 | tf_op jit(solution)/shard_map/ppermute | solution.py:138
  156.2 3.6 %collective-permute-done.23 = bf16[24,7168]{1,0:T(8,128)(2,1)S(1)} collective-permute-done((bf16[24,7168]{1,0:T(8,128)(2,1)S(1)}, bf16[24,7168]{1,0:T(8,128)(2,1)S(1)}, u32[]{:S(2)}, u32[]{:S(2)}) %collective-permute-start.23) | collective-permute-done | bytes 344096 | tf_op jit(solution)/shard_map/ppermute | solution.py:138
  162.4 3.6 %collective-permute-done.30 = bf16[40,7168]{1,0:T(8,128)(2,1)S(1)} collective-permute-done((bf16[40,7168]{1,0:T(8,128)(2,1)S(1)}, bf16[40,7168]{1,0:T(8,128)(2,1)S(1)}, u32[]{:S(2)}, u32[]{:S(2)}) %collective-permute-start.30) | collective-permute-done | bytes 573472 | tf_op jit(solution)/shard_map/ppermute | solution.py:138
  168.5 16.0 %collective-permute-done.31 = bf16[40,7168]{1,0:T(8,128)(2,1)S(1)} collective-permute-done((bf16[40,7168]{1,0:T(8,128)(2,1)S(1)}, bf16[40,7168]{1,0:T(8,128)(2,1)S(1)}, u32[]{:S(2)}, u32[]{:S(2)}) %collective-permute-start.31) | collective-permute-done | bytes 573472 | tf_op jit(solution)/shard_map/ppermute | solution.py:138
  187.6 3.3 %collective-permute-start.26 = (bf16[24,7168]{1,0:T(8,128)(2,1)S(1)}, bf16[24,7168]{1,0:T(8,128)(2,1)S(1)}, u32[]{:S(2)}, u32[]{:S(2)}) collective-permute-start(bf16[24,7168]{1,0:T(8,128)(2,1)S(1)} %add_convert_fusion.7), channel_id=1, source_target_pairs={{0,14},{1,113},{2,0},{3,115},{4,2},{5,117},{6,4},{7,119},{8,6},{9,... | collective-permute-start | bytes 1032200 | tf_op jit(solution)/shard_map/ppermute | solution.py:138
  190.9 4.4 %collective-permute-done.33 = bf16[40,7168]{1,0:T(8,128)(2,1)S(1)} collective-permute-done((bf16[40,7168]{1,0:T(8,128)(2,1)S(1)}, bf16[40,7168]{1,0:T(8,128)(2,1)S(1)}, u32[]{:S(2)}, u32[]{:S(2)}) %collective-permute-start.33) | collective-permute-done | bytes 573472 | tf_op jit(solution)/shard_map/ppermute | solution.py:138
  195.3 3.4 %collective-permute-done.34 = bf16[40,7168]{1,0:T(8,128)(2,1)S(1)} collective-permute-done((bf16[40,7168]{1,0:T(8,128)(2,1)S(1)}, bf16[40,7168]{1,0:T(8,128)(2,1)S(1)}, u32[]{:S(2)}, u32[]{:S(2)}) %collective-permute-start.34) | collective-permute-done | bytes 573472 | tf_op jit(solution)/shard_map/ppermute | solution.py:138
  199.3 8.7 %collective-permute-done.36 = bf16[16,7168]{1,0:T(8,128)(2,1)S(1)} collective-permute-done((bf16[16,7168]{1,0:T(8,128)(2,1)S(1)}, bf16[16,7168]{1,0:T(8,128)(2,1)S(1)}, u32[]{:S(2)}, u32[]{:S(2)}) %collective-permute-start.36) | collective-permute-done | bytes 229408 | tf_op jit(solution)/shard_map/ppermute | solution.py:141
  208.0 4.1 %collective-permute-done.35 = bf16[24,7168]{1,0:T(8,128)(2,1)S(1)} collective-permute-done((bf16[24,7168]{1,0:T(8,128)(2,1)S(1)}, bf16[24,7168]{1,0:T(8,128)(2,1)S(1)}, u32[]{:S(2)}, u32[]{:S(2)}) %collective-permute-start.35) | collective-permute-done | bytes 344096 | tf_op jit(solution)/shard_map/ppermute | solution.py:141
  (114 shorter events, 57.6 us)
Async XLA Ops:
  3.0 21.9 %collective-permute-start.1 = (bf16[8,7296]{1,0:T(8,128)(2,1)S(1)}, bf16[8,7296]{1,0:T(8,128)(2,1)S(1)}, u32[]{:S(2)}, u32[]{:S(2)}) collective-permute-start(bf16[8,7296]{1,0:T(8,128)(2,1)S(1)} %pad_maximum_fusion.2), channel_id=1, source_target_pairs={{0,112},{1,15},{2,114},{3,1},{4,116},{5,3},{6,118},{7,5},{8,120},{... | collective-permute-start | bytes 350216 | tf_op jit(solution)/shard_map/ppermute | solution.py:141
  28.3 20.9 %collective-permute-start.2 = (bf16[24,7296]{1,0:T(8,128)(2,1)S(1)}, bf16[24,7296]{1,0:T(8,128)(2,1)S(1)}, u32[]{:S(2)}, u32[]{:S(2)}) collective-permute-start(bf16[24,7296]{1,0:T(8,128)(2,1)S(1)} %pad_maximum_fusion.refs_0_), channel_id=1, source_target_pairs={{0,48},{1,7},{2,50},{3,9},{4,52},{5,11},{6,54},{7,13},{8,56},{9,15... | collective-permute-start | bytes 1050632 | tf_op jit(solution)/shard_map/ppermute | solution.py:141
  29.4 10.8 %collective-permute-start.3 = (bf16[16,7296]{1,0:T(8,128)(2,1)S(1)}, bf16[16,7296]{1,0:T(8,128)(2,1)S(1)}, u32[]{:S(2)}, u32[]{:S(2)}) collective-permute-start(bf16[16,7296]{1,0:T(8,128)(2,1)S(1)} %pad_maximum_fusion.1), channel_id=1, source_target_pairs={{0,96},{1,13},{2,98},{3,15},{4,100},{5,1},{6,102},{7,3},{8,104},{9... | collective-permute-start | bytes 700424 | tf_op jit(solution)/shard_map/ppermute | solution.py:141
  33.0 83.8 %collective-permute-start.8 = (bf16[2,7168,128]{2,1,0:T(8,128)(2,1)}, bf16[2,7168,128]{2,1,0:T(8,128)(2,1)}, u32[]{:S(2)}, u32[]{:S(2)}) collective-permute-start(bf16[2,7168,128]{2,1,0:T(8,128)(2,1)} %refs_10_.3), channel_id=1, source_target_pairs={{0,1},{1,0},{2,3},{3,2},{4,5},{5,4},{6,7},{7,6},{8,9},{9,8},{10,11... | collective-permute-start | bytes 11010056 | tf_op jit(solution)/shard_map/ppermute | solution.py:163
  33.0 83.8 %collective-permute-start.9 = (bf16[2,7168,128]{2,1,0:T(8,128)(2,1)}, bf16[2,7168,128]{2,1,0:T(8,128)(2,1)}, u32[]{:S(2)}, u32[]{:S(2)}) collective-permute-start(bf16[2,7168,128]{2,1,0:T(8,128)(2,1)} %refs_11_.1), channel_id=1, source_target_pairs={{0,1},{1,0},{2,3},{3,2},{4,5},{5,4},{6,7},{7,6},{8,9},{9,8},{10,11... | collective-permute-start | bytes 11010056 | tf_op jit(solution)/shard_map/ppermute | solution.py:163
  33.5 83.3 %collective-permute-start.10 = (bf16[2,128,7168]{2,1,0:T(8,128)(2,1)}, bf16[2,128,7168]{2,1,0:T(8,128)(2,1)}, u32[]{:S(2)}, u32[]{:S(2)}) collective-permute-start(bf16[2,128,7168]{2,1,0:T(8,128)(2,1)} %refs_14_.1), channel_id=1, source_target_pairs={{0,1},{1,0},{2,3},{3,2},{4,5},{5,4},{6,7},{7,6},{8,9},{9,8},{10,11... | collective-permute-start | bytes 11010056 | tf_op jit(solution)/shard_map/ppermute | solution.py:163
  49.3 9.9 %collective-permute-start.7 = (bf16[40,7296]{1,0:T(8,128)(2,1)S(1)}, bf16[40,7296]{1,0:T(8,128)(2,1)S(1)}, u32[]{:S(2)}, u32[]{:S(2)}) collective-permute-start(bf16[40,7296]{1,0:T(8,128)(2,1)S(1)} %constant_dynamic-update-slice_fusion.refs_1_), channel_id=1, source_target_pairs={{0,14},{1,113},{2,0},{3,115},{4,2},{5,117},{6,4},{7,119},{8,6},{9,... | collective-permute-start | bytes 1751048 | tf_op jit(solution)/shard_map/ppermute | solution.py:138
  49.4 11.1 %collective-permute-start.6 = (bf16[40,7296]{1,0:T(8,128)(2,1)S(1)}, bf16[40,7296]{1,0:T(8,128)(2,1)S(1)}, u32[]{:S(2)}, u32[]{:S(2)}) collective-permute-start(bf16[40,7296]{1,0:T(8,128)(2,1)S(1)} %constant_dynamic-update-slice_fusion.refs_1_), channel_id=1, source_target_pairs={{0,2},{1,17},{2,4},{3,19},{4,6},{5,21},{6,8},{7,23},{8,10},{9,25},... | collective-permute-start | bytes 1751048 | tf_op jit(solution)/shard_map/ppermute | solution.py:138
  66.5 11.0 %collective-permute-start.13 = (bf16[40,7296]{1,0:T(8,128)(2,1)S(1)}, bf16[40,7296]{1,0:T(8,128)(2,1)S(1)}, u32[]{:S(2)}, u32[]{:S(2)}) collective-permute-start(bf16[40,7296]{1,0:T(8,128)(2,1)S(1)} %collective-permute-done.6.refs_3_), channel_id=1, source_target_pairs={{0,2},{1,17},{2,4},{3,19},{4,6},{5,21},{6,8},{7,23},{8,10},{9,25},... | collective-permute-start | bytes 1751048 | tf_op jit(solution)/shard_map/ppermute | solution.py:138
  86.1 11.0 %collective-permute-start.17 = (bf16[40,7296]{1,0:T(8,128)(2,1)S(1)}, bf16[40,7296]{1,0:T(8,128)(2,1)S(1)}, u32[]{:S(2)}, u32[]{:S(2)}) collective-permute-start(bf16[40,7296]{1,0:T(8,128)(2,1)S(1)} %collective-permute-done.13.refs_1_), channel_id=1, source_target_pairs={{0,2},{1,17},{2,4},{3,19},{4,6},{5,21},{6,8},{7,23},{8,10},{9,25},... | collective-permute-start | bytes 1751048 | tf_op jit(solution)/shard_map/ppermute | solution.py:138
  86.4 12.4 %collective-permute-start.18 = (bf16[40,7296]{1,0:T(8,128)(2,1)S(1)}, bf16[40,7296]{1,0:T(8,128)(2,1)}, u32[]{:S(2)}, u32[]{:S(2)}) collective-permute-start(bf16[40,7296]{1,0:T(8,128)(2,1)S(1)} %collective-permute-done.14.refs_3_), channel_id=1, source_target_pairs={{0,14},{1,113},{2,0},{3,115},{4,2},{5,117},{6,4},{7,119},{8,6},{9,... | collective-permute-start | bytes 1751048 | tf_op jit(solution)/shard_map/ppermute | solution.py:138
  106.6 10.2 %collective-permute-start.20 = (bf16[40,7296]{1,0:T(8,128)(2,1)}, bf16[40,7296]{1,0:T(8,128)(2,1)}, u32[]{:S(2)}, u32[]{:S(2)}) collective-permute-start(bf16[40,7296]{1,0:T(8,128)(2,1)} %collective-permute-done.18.refs_7_), channel_id=1, source_target_pairs={{0,14},{1,113},{2,0},{3,115},{4,2},{5,117},{6,4},{7,119},{8,6},{9,... | collective-permute-start | bytes 1751048 | tf_op jit(solution)/shard_map/ppermute | solution.py:138
  137.5 10.5 %collective-permute-start.21 = (bf16[24,7168]{1,0:T(8,128)(2,1)S(1)}, bf16[24,7168]{1,0:T(8,128)(2,1)S(1)}, u32[]{:S(2)}, u32[]{:S(2)}) collective-permute-start(bf16[24,7168]{1,0:T(8,128)(2,1)S(1)} %get-tuple-element.69), channel_id=1, source_target_pairs={{0,14},{1,113},{2,0},{3,115},{4,2},{5,117},{6,4},{7,119},{8,6},{9,... | collective-permute-start | bytes 1032200 | tf_op jit(solution)/shard_map/ppermute | solution.py:138
  139.6 11.8 %collective-permute-start.28 = (bf16[40,7168]{1,0:T(8,128)(2,1)S(1)}, bf16[40,7168]{1,0:T(8,128)(2,1)S(1)}, u32[]{:S(2)}, u32[]{:S(2)}) collective-permute-start(bf16[40,7168]{1,0:T(8,128)(2,1)S(1)} %get-tuple-element.84), channel_id=1, source_target_pairs={{0,2},{1,17},{2,4},{3,19},{4,6},{5,21},{6,8},{7,23},{8,10},{9,25},... | collective-permute-start | bytes 1720328 | tf_op jit(solution)/shard_map/ppermute | solution.py:138
  151.5 10.8 %collective-permute-start.29 = (bf16[40,7168]{1,0:T(8,128)(2,1)S(1)}, bf16[40,7168]{1,0:T(8,128)(2,1)S(1)}, u32[]{:S(2)}, u32[]{:S(2)}) collective-permute-start(bf16[40,7168]{1,0:T(8,128)(2,1)S(1)} %get-tuple-element.85), channel_id=1, source_target_pairs={{0,14},{1,113},{2,0},{3,115},{4,2},{5,117},{6,4},{7,119},{8,6},{9,... | collective-permute-start | bytes 1720328 | tf_op jit(solution)/shard_map/ppermute | solution.py:138
  154.9 11.1 %collective-permute-start.30 = (bf16[40,7168]{1,0:T(8,128)(2,1)S(1)}, bf16[40,7168]{1,0:T(8,128)(2,1)S(1)}, u32[]{:S(2)}, u32[]{:S(2)}) collective-permute-start(bf16[40,7168]{1,0:T(8,128)(2,1)S(1)} %add_convert_fusion.5), channel_id=1, source_target_pairs={{0,2},{1,17},{2,4},{3,19},{4,6},{5,21},{6,8},{7,23},{8,10},{9,25},... | collective-permute-start | bytes 1720328 | tf_op jit(solution)/shard_map/ppermute | solution.py:138
  160.1 27.4 %collective-permute-start.25 = (bf16[24,7168]{1,0:T(8,128)(2,1)S(1)}, bf16[24,7168]{1,0:T(8,128)(2,1)S(1)}, u32[]{:S(2)}, u32[]{:S(2)}) collective-permute-start(bf16[24,7168]{1,0:T(8,128)(2,1)S(1)} %add_convert_fusion.8), channel_id=1, source_target_pairs={{0,2},{1,17},{2,4},{3,19},{4,6},{5,21},{6,8},{7,23},{8,10},{9,25},... | collective-permute-start | bytes 1032200 | tf_op jit(solution)/shard_map/ppermute | solution.py:138
  166.1 18.3 %collective-permute-start.31 = (bf16[40,7168]{1,0:T(8,128)(2,1)S(1)}, bf16[40,7168]{1,0:T(8,128)(2,1)S(1)}, u32[]{:S(2)}, u32[]{:S(2)}) collective-permute-start(bf16[40,7168]{1,0:T(8,128)(2,1)S(1)} %add_convert_fusion.4), channel_id=1, source_target_pairs={{0,14},{1,113},{2,0},{3,115},{4,2},{5,117},{6,4},{7,119},{8,6},{9,... | collective-permute-start | bytes 1720328 | tf_op jit(solution)/shard_map/ppermute | solution.py:138
  167.4 17.2 %collective-permute-start.32 = (bf16[40,7168]{1,0:T(8,128)(2,1)S(1)}, bf16[40,7168]{1,0:T(8,128)(2,1)S(1)}, u32[]{:S(2)}, u32[]{:S(2)}) collective-permute-start(bf16[40,7168]{1,0:T(8,128)(2,1)S(1)} %add_convert_fusion.3), channel_id=1, source_target_pairs={{0,2},{1,17},{2,4},{3,19},{4,6},{5,21},{6,8},{7,23},{8,10},{9,25},... | collective-permute-start | bytes 1720328 | tf_op jit(solution)/shard_map/ppermute | solution.py:138
  184.7 10.6 %collective-permute-start.33 = (bf16[40,7168]{1,0:T(8,128)(2,1)S(1)}, bf16[40,7168]{1,0:T(8,128)(2,1)S(1)}, u32[]{:S(2)}, u32[]{:S(2)}) collective-permute-start(bf16[40,7168]{1,0:T(8,128)(2,1)S(1)} %add_convert_fusion.2), channel_id=1, source_target_pairs={{0,14},{1,113},{2,0},{3,115},{4,2},{5,117},{6,4},{7,119},{8,6},{9,... | collective-permute-start | bytes 1720328 | tf_op jit(solution)/shard_map/ppermute | solution.py:138
  187.5 11.2 %collective-permute-start.34 = (bf16[40,7168]{1,0:T(8,128)(2,1)S(1)}, bf16[40,7168]{1,0:T(8,128)(2,1)S(1)}, u32[]{:S(2)}, u32[]{:S(2)}) collective-permute-start(bf16[40,7168]{1,0:T(8,128)(2,1)S(1)} %add_convert_fusion.1), channel_id=1, source_target_pairs={{0,2},{1,17},{2,4},{3,19},{4,6},{5,21},{6,8},{7,23},{8,10},{9,25},... | collective-permute-start | bytes 1720328 | tf_op jit(solution)/shard_map/ppermute | solution.py:138
  187.6 20.4 %collective-permute-start.26 = (bf16[24,7168]{1,0:T(8,128)(2,1)S(1)}, bf16[24,7168]{1,0:T(8,128)(2,1)S(1)}, u32[]{:S(2)}, u32[]{:S(2)}) collective-permute-start(bf16[24,7168]{1,0:T(8,128)(2,1)S(1)} %add_convert_fusion.7), channel_id=1, source_target_pairs={{0,14},{1,113},{2,0},{3,115},{4,2},{5,117},{6,4},{7,119},{8,6},{9,... | collective-permute-start | bytes 1032200 | tf_op jit(solution)/shard_map/ppermute | solution.py:138
  190.9 17.1 %collective-permute-start.27 = (bf16[24,7168]{1,0:T(8,128)(2,1)S(1)}, bf16[24,7168]{1,0:T(8,128)(2,1)S(1)}, u32[]{:S(2)}, u32[]{:S(2)}) collective-permute-start(bf16[24,7168]{1,0:T(8,128)(2,1)S(1)} %add_convert_fusion.6), channel_id=1, source_target_pairs={{0,2},{1,17},{2,4},{3,19},{4,6},{5,21},{6,8},{7,23},{8,10},{9,25},... | collective-permute-start | bytes 1032200 | tf_op jit(solution)/shard_map/ppermute | solution.py:138
  199.0 13.1 %collective-permute-start.35 = (bf16[24,7168]{1,0:T(8,128)(2,1)S(1)}, bf16[24,7168]{1,0:T(8,128)(2,1)S(1)}, u32[]{:S(2)}, u32[]{:S(2)}) collective-permute-start(bf16[24,7168]{1,0:T(8,128)(2,1)S(1)} %slice.31), channel_id=1, source_target_pairs={{0,80},{1,11},{2,82},{3,13},{4,84},{5,15},{6,86},{7,1},{8,88},{9,3... | collective-permute-start | bytes 1032200 | tf_op jit(solution)/shard_map/ppermute | solution.py:141
  (31 other events, 186.3 us)
